TPU v7x, 16 devices: a whole 2x2x2 slice. The times are simulated.
16 devices in a mesh: dp: 2 (over z), tp: 8 (over y, x, core).
Axes of the slice: x: 2, y: 2, z: 2, core: 2. Of those that a mesh axis runs over, the one named last changes fastest.
Arguments:
- act_in: bfloat16 [16, 512, 5120], P('dp'), parts along dimension 0
- ln_gain: float32 [2, 5120], replicated
- ln_bias: float32 [2, 5120], replicated
- w_qkv: bfloat16 [2, 5120, 40, 384], P(None, None, 'tp')
- w_out: bfloat16 [2, 5120, 5120], P(None, 'tp')
- w_up: bfloat16 [2, 5120, 20480], P(None, None, 'tp')
- w_down: bfloat16 [2, 20480, 5120], P(None, 'tp')
Outputs:
- output: bfloat16 [16, 512, 5120], P('dp'), parts along dimension 0
There are 2 independent parts. A program takes and returns all parts, laid end to end along the dimension named above; an argument that names none is the same for every part.
All inputs are finite; a program needn't handle non-finite values.
Results may differ from a plain program's by a relative error of at most 0.0169081.
Values are sent between devices in bfloat16 or wider.
A program may use at most 1 GiB of HBM per device.

v0:
```python
import jax
import jax.numpy as jnp
from jax import lax
from jax.sharding import PartitionSpec as P

LN_EPS = 1e-5
ROPE_BASE = 10000.0


def layer_norm(hidden, gain, bias):
    hidden_f = hidden.astype(jnp.float32)
    row_mean = jnp.mean(hidden_f, axis=-1, keepdims=True)
    centered = hidden_f - row_mean
    row_var = jnp.mean(centered * centered, axis=-1, keepdims=True)
    return (centered * lax.rsqrt(row_var + LN_EPS) * gain + bias).astype(jnp.bfloat16)


def rope_tables(seq_len, head_dim):
    half_dim = head_dim // 2
    inv_freq = ROPE_BASE ** (-2.0 * jnp.arange(half_dim, dtype=jnp.float32) / head_dim)
    angles = jnp.arange(seq_len, dtype=jnp.float32)[:, None] * inv_freq[None, :]
    return jnp.cos(angles), jnp.sin(angles)


def apply_rope(proj, cos_tab, sin_tab):
    half_dim = proj.shape[-1] // 2
    first = proj[..., :half_dim]
    second = proj[..., half_dim:]
    return jnp.concatenate([first * cos_tab - second * sin_tab, second * cos_tab + first * sin_tab], axis=-1)


def layer_partial(hidden, gain, bias, w_qkv, w_out, w_up, w_down):
    batch, seq_len, d_model = hidden.shape
    groups = w_qkv.shape[1]
    attn_width = w_out.shape[0]
    head_dim = (w_qkv.shape[2] - attn_width // groups) // 2
    group_heads = attn_width // (groups * head_dim)
    normed = layer_norm(hidden, gain, bias)
    qkv_proj = jnp.einsum("bsd,dgc->bsgc", normed, w_qkv, preferred_element_type=jnp.float32)
    qkv_proj = qkv_proj.reshape(batch, seq_len, groups, group_heads + 2, head_dim)
    cos_tab, sin_tab = rope_tables(seq_len, head_dim)
    query = apply_rope(qkv_proj[:, :, :, :group_heads], cos_tab[None, :, None, None, :], sin_tab[None, :, None, None, :]).astype(jnp.bfloat16)
    keys = apply_rope(qkv_proj[:, :, :, group_heads], cos_tab[None, :, None, :], sin_tab[None, :, None, :]).astype(jnp.bfloat16)
    values = qkv_proj[:, :, :, group_heads + 1].astype(jnp.bfloat16)
    scores = jnp.einsum("bsgrd,btgd->bgrst", query, keys, preferred_element_type=jnp.float32) * (head_dim ** -0.5)
    positions = jnp.arange(seq_len)
    allowed = positions[:, None] >= positions[None, :]
    scores = jnp.where(allowed, scores, -1e30)
    attn_probs = jax.nn.softmax(scores, axis=-1).astype(jnp.bfloat16)
    context = jnp.einsum("bgrst,btgd->bgrsd", attn_probs, values, preferred_element_type=jnp.float32).astype(jnp.bfloat16)
    out_heads = w_out.reshape(groups, group_heads, head_dim, d_model)
    attn_part = jnp.einsum("bgrsd,grde->bse", context, out_heads, preferred_element_type=jnp.float32)
    up_proj = jnp.einsum("bsd,df->bsf", normed, w_up, preferred_element_type=jnp.float32)
    gelu_out = jax.nn.gelu(up_proj, approximate=False).astype(jnp.bfloat16)
    mlp_part = jnp.einsum("bsf,fe->bse", gelu_out, w_down, preferred_element_type=jnp.float32)
    return attn_part + mlp_part


def solution(mesh):
    def shard_body(act_in, ln_gain, ln_bias, w_qkv, w_out, w_up, w_down):
        hidden = act_in
        for layer_idx in range(ln_gain.shape[0]):
            local_sum = layer_partial(hidden, ln_gain[layer_idx], ln_bias[layer_idx], w_qkv[layer_idx], w_out[layer_idx], w_up[layer_idx], w_down[layer_idx]).astype(jnp.bfloat16)
            reduced = lax.psum(local_sum, "tp")
            hidden = (hidden.astype(jnp.float32) + reduced.astype(jnp.float32)).astype(jnp.bfloat16)
        return hidden

    return jax.shard_map(shard_body, mesh=mesh, in_specs=(P("dp", None, None), P(None, None), P(None, None), P(None, None, "tp", None), P(None, "tp", None), P(None, None, "tp"), P(None, "tp", None)), out_specs=P("dp", None, None), check_vma=False)
```

profile of v0, /device:TPU:0, one launch (start us, length us, event | category | flops | bytes accessed | tf_op | source)
XLA Modules:
  0.0 2315.3 jit_solution(9381354107857623938)
XLA Ops:
  6.5 0.0 all-reduce.3.cloned.1.call-start
  6.5 0.8 iota_compare_fusion
  7.3 0.0 copy-start.11
  7.3 0.0 copy-start.12
  7.3 13.8 convert_reduce_fusion.1
  21.1 15.9 fusion.8
  37.1 0.0 copy-done.11
  37.1 0.6 fusion.255
  37.7 0.0 copy-done.12
  37.7 0.6 fusion.256
  38.4 1.3 fusion.180
  39.6 27.6 %slice_bitcast_fusion = (bf16[5,384,5120]{1,2,0:T(8,128)(2,1)}, bf16[5,384,5120]{1,2,0:T(8,128)(2,1)}) fusion(bf16[2,5120,5,384]{3,1,2,0:T(8,128)(2,1)} %param.10), kind=kLoop, calls=%fused_computation.159 | loop fusion | bytes 78643200 | tf_op jit(solution)/shard_map/bsd,dgc->bsgc/dot_general | solution.py:39
  67.2 24.1 %copy.8 = bf16[5,384,5120]{2,1,0:T(8,128)(2,1)} copy(bf16[5,384,5120]{1,2,0:T(8,128)(2,1)} %get-tuple-element.12) | data formatting | bytes 39321600 | tf_op jit(solution)/shard_map/bsd,dgc->bsgc/dot_general | solution.py:39
  91.3 0.0 copy-start
  91.3 96.7 %fusion.24 = f32[8,512,5,3,128]{1,4,3,2,0:T(8,128)} fusion(bf16[5,3,128,5120,1]{3,2,1,0,4:T(8,128)(2,1)} %bitcast.231, bf16[8,512,5120]{2,1,0:T(8,128)(2,1)} %param.7, f32[5120]{0:T(1024)S(1)} %bitcast.240, f32[5120]{0:T(1024)S(1)} %bitcast.238, f32[8,512]{1,0:T(8,128)S(1)} %add_rsqrt_fusion.1, f32[8,512]{1,0:T(8,128)S(1)} %broadcast_multiply_fusion.1), kind=kOutput, calls=%fused_computation.45 | convolution fusion | flops 80656465920 | bytes 93134848 | tf_op jit(solution)/shard_map/bsd,dgc->bsgc/dot_general | solution.py:39
  188.1 0.0 copy-done
  188.1 0.0 copy-done.3
  188.1 0.0 copy-start.7
  188.1 5.6 fusion.178
  193.7 7.2 fusion.177
  200.9 5.5 slice_bitcast_fusion.3
  206.4 10.4 fusion.254
  216.8 3.3 subtract_convert_fusion.2
  220.2 0.0 copy-done.7
  220.2 18.4 fusion.40
  238.6 17.7 fusion.38
  256.3 23.0 fusion.293
  279.3 131.3 %fusion.128 = (u8[512,2560]{1,0:T(8,128)(4,1)S(1)}, u8[512,2560]{1,0:T(8,128)(4,1)S(1)}, f32[8,512,2560]{2,1,0:T(8,128)}) fusion(bf16[2,5120,2560]{2,1,0:T(8,128)(2,1)} %param.12, bf16[8,512,5120]{2,1,0:T(8,128)(2,1)} %param.7, f32[5120]{0:T(1024)S(1)} %bitcast.241, f32[5120]{0:T(1024)S(1)} %bitcast.239, f32[8,512]{1,0:T(8,128)S(1)} %add_rsqrt_fusion.1, ...), kind=kOutput, calls=%fused_computation.167 | convolution fusion | flops 107633704960 | bytes 112795648 | tf_op jit(solution)/shard_map/bsd,df->bsf/dot_general | solution.py:53
  410.6 42.1 %fusion.165 = f32[8,512,5120,1]{2,1,3,0:T(8,128)} fusion(bf16[5,128,5120,1]{2,1,0,3:T(8,128)(2,1)} %bitcast.233, bf16[8,5,512,128]{3,2,1,0:T(8,128)(2,1)} %fusion.293), kind=kOutput, calls=%fused_computation.204 | convolution fusion | flops 26843545600 | bytes 95682560 | tf_op jit(solution)/shard_map/bgrsd,grde->bse/dot_general | solution.py:52
  452.7 97.3 %fusion.285 = bf16[8,512,2560]{2,1,0:T(8,128)(2,1)} fusion(f32[8,512,2560]{2,1,0:T(8,128)} %get-tuple-element.29, u8[512,2560]{1,0:T(8,128)(4,1)S(1)} %get-tuple-element.8, u8[512,2560]{1,0:T(8,128)(4,1)S(1)} %get-tuple-element.7), kind=kLoop, calls=%fused_computation.28.clone.clone.2 | loop fusion | flops 734003200 | bytes 65536000 | tf_op jit(solution)/shard_map/bsf,fe->bse/dot_general | solution.py:55
  550.0 124.5 %fusion.15 = bf16[8,512,5120]{2,1,0:T(8,128)(2,1)} fusion(f32[8,512,5120,1]{2,1,3,0:T(8,128)} %fusion.165, bf16[2,2560,5120]{2,1,0:T(8,128)(2,1)} %param.13, bf16[8,512,2560]{2,1,0:T(8,128)(2,1)} %fusion.285), kind=kOutput, calls=%fused_computation.23 | convolution fusion | flops 107416125440 | bytes 173015040 | tf_op jit(solution)/shard_map/bsf,fe->bse/dot_general | solution.py:55
  674.5 0.0 all-reduce.3.cloned.1.call-update
  674.5 0.0 all-reduce.5.cloned.1.call-start
  674.6 26.1 %copy.15 = bf16[5,384,5120]{2,1,0:T(8,128)(2,1)} copy(bf16[5,384,5120]{1,2,0:T(8,128)(2,1)} %get-tuple-element.11) | data formatting | bytes 39321600 | tf_op jit(solution)/shard_map/bsd,dgc->bsgc/dot_general | solution.py:39
  700.7 456.8 %all-reduce.3.cloned.1.call-done = bf16[8,512,5120]{2,1,0:T(8,128)(2,1)} async-done(((bf16[8,512,5120]{2,1,0:T(8,128)(2,1)}), bf16[8,512,5120]{2,1,0:T(8,128)(2,1)}) %all-reduce.3.cloned.1.call-update) | async-done | bytes 41943056 | tf_op jit(solution)/shard_map/psum | solution.py:64
  1157.5 41.0 %convert_reduce_fusion = (f32[8,512]{1,0:T(8,128)S(1)}, bf16[8,512,5120]{2,1,0:T(8,128)(2,1)}) fusion(bf16[8,512,5120]{2,1,0:T(8,128)(2,1)} %all-reduce.3.cloned.1.call-done, bf16[8,512,5120]{2,1,0:T(8,128)(2,1)} %param.7), kind=kLoop, calls=%fused_computation.2 | loop fusion | flops 125825024 | bytes 125845504 | tf_op jit(solution)/shard_map/reduce_sum | solution.py:12
  1198.5 0.0 copy-start.14
  1198.5 15.9 fusion.4
  1214.5 0.0 copy-done.13
  1214.5 0.0 copy-done.14
  1214.5 0.0 copy-start.1
  1214.5 0.0 copy-start.4
  1214.5 96.1 %fusion.22 = f32[8,512,5,3,128]{1,4,3,2,0:T(8,128)} fusion(bf16[5,3,128,5120,1]{3,2,1,0,4:T(8,128)(2,1)} %bitcast.230, bf16[8,512,5120]{2,1,0:T(8,128)(2,1)} %get-tuple-element.10, f32[5120]{0:T(1024)S(1)} %bitcast.236, f32[5120]{0:T(1024)S(1)} %bitcast.234, f32[8,512]{1,0:T(8,128)S(1)} %add_rsqrt_fusion, f32[8,512]{1,0:T(8,128)S(1)} %broadcast_multiply_fusion), kind=kOutput, calls=%fused_computation.42 | convolution fusion | flops 80656465920 | bytes 93134848 | tf_op jit(solution)/shard_map/bsd,dgc->bsgc/dot_general | solution.py:39
  1310.6 0.0 copy-done.1
  1310.6 0.0 copy-done.4
  1310.6 6.7 fusion.175
  1317.3 10.1 slice_bitcast_fusion.2
  1327.4 132.3 %fusion.129 = (u8[512,2560]{1,0:T(8,128)(4,1)}, u8[512,2560]{1,0:T(8,128)(4,1)}, f32[8,512,2560]{2,1,0:T(8,128)}) fusion(bf16[2,5120,2560]{2,1,0:T(8,128)(2,1)} %param.12, bf16[8,512,5120]{2,1,0:T(8,128)(2,1)} %get-tuple-element.10, f32[5120]{0:T(1024)S(1)} %bitcast.237, f32[5120]{0:T(1024)S(1)} %bitcast.235, f32[8,512]{1,0:T(8,128)S(1)} %add_rsqrt_fusion, ...), kind=kOutput, calls=%fused_computation.168 | convolution fusion | flops 107633704960 | bytes 112795648 | tf_op jit(solution)/shard_map/bsd,df->bsf/dot_general | solution.py:53
  1459.7 0.0 copy-done.2
  1459.7 0.0 copy-done.5
  1459.7 5.0 subtract_convert_fusion.1
  1464.7 0.0 copy-done.6
  1464.7 0.0 copy-done.8
  1464.7 16.9 fusion.41
  1481.7 17.7 fusion.39
  1499.4 23.1 fusion.289
  1522.5 42.0 %fusion.155 = f32[8,512,5120,1]{2,1,3,0:T(8,128)} fusion(bf16[5,128,5120,1]{2,1,0,3:T(8,128)(2,1)} %bitcast.232, bf16[8,5,512,128]{3,2,1,0:T(8,128)(2,1)} %fusion.289), kind=kOutput, calls=%fused_computation.198 | convolution fusion | flops 26843545600 | bytes 95682560 | tf_op jit(solution)/shard_map/bgrsd,grde->bse/dot_general | solution.py:52
  1564.5 0.0 copy-done.9
  1564.5 0.0 copy-done.10
  1564.5 97.3 %fusion.283 = bf16[8,512,2560]{2,1,0:T(8,128)(2,1)} fusion(f32[8,512,2560]{2,1,0:T(8,128)} %get-tuple-element.32, u8[512,2560]{1,0:T(8,128)(4,1)S(1)} %copy-done.10, u8[512,2560]{1,0:T(8,128)(4,1)S(1)} %copy-done.9), kind=kLoop, calls=%fused_computation.31.clone.clone.2 | loop fusion | flops 734003200 | bytes 65536000 | tf_op jit(solution)/shard_map/bsf,fe->bse/dot_general | solution.py:55
  1661.9 124.8 %fusion.14 = bf16[8,512,5120]{2,1,0:T(8,128)(2,1)} fusion(f32[8,512,5120,1]{2,1,3,0:T(8,128)} %fusion.155, bf16[2,2560,5120]{2,1,0:T(8,128)(2,1)} %param.13, bf16[8,512,2560]{2,1,0:T(8,128)(2,1)} %fusion.283), kind=kOutput, calls=%fused_computation.21 | convolution fusion | flops 107416125440 | bytes 173015040 | tf_op jit(solution)/shard_map/bsf,fe->bse/dot_general | solution.py:55
  1786.7 0.0 all-reduce.5.cloned.1.call-update
  1786.7 480.1 %all-reduce.5.cloned.1.call-done = bf16[8,512,5120]{2,1,0:T(8,128)(2,1)} async-done(((bf16[8,512,5120]{2,1,0:T(8,128)(2,1)}), bf16[8,512,5120]{2,1,0:T(8,128)(2,1)}) %all-reduce.5.cloned.1.call-update) | async-done | bytes 41943056 | tf_op jit(solution)/shard_map/psum | solution.py:64
  2266.8 41.4 %fusion.13 = bf16[8,512,5120]{2,1,0:T(8,128)(2,1)} fusion(bf16[8,512,5120]{2,1,0:T(8,128)(2,1)} %get-tuple-element.10, bf16[8,512,5120]{2,1,0:T(8,128)(2,1)} %all-reduce.5.cloned.1.call-done), kind=kLoop, calls=%fused_computation.19 | loop fusion | flops 83886080 | bytes 125829120 | tf_op jit(solution)/shard_map/convert_element_type | solution.py:65
  (13 shorter events, 0.1 us)
Async XLA Ops:
  6.5 1150.9 %all-reduce.3.cloned.1.call-start = ((), (), s32[]{:S(2)}) async-start(), calls=%async_computation | async-start | bytes 83886080 | tf_op jit(solution)/shard_map/psum | solution.py:64
  7.3 29.7 %copy-start.11 = (f32[2,5120]{1,0:T(2,128)S(1)}, f32[2,5120]{1,0:T(2,128)}, u32[]{:S(2)}) copy-start(f32[2,5120]{1,0:T(2,128)} %param.8) | copy-start | bytes 122884
  7.3 30.4 %copy-start.12 = (f32[2,5120]{1,0:T(2,128)S(1)}, f32[2,5120]{1,0:T(2,128)}, u32[]{:S(2)}) copy-start(f32[2,5120]{1,0:T(2,128)} %param.9) | copy-start | bytes 122884
  91.3 96.8 %copy-start = (f32[512,64]{0,1:T(8,128)S(1)}, f32[512,64]{0,1:T(8,128)}, u32[]{:S(2)}) copy-start(f32[512,64]{0,1:T(8,128)} %get-tuple-element.25) | copy-start | bytes 393220
  91.3 96.8 %copy-start.3 = (f32[512,64]{0,1:T(8,128)S(1)}, f32[512,64]{0,1:T(8,128)}, u32[]{:S(2)}) copy-start(f32[512,64]{0,1:T(8,128)} %get-tuple-element.26) | copy-start | bytes 393220
  188.1 32.0 %copy-start.7 = (pred[512,512]{0,1:T(8,128)(4,1)S(1)}, pred[512,512]{0,1:T(8,128)(4,1)}, u32[]{:S(2)}) copy-start(pred[512,512]{0,1:T(8,128)(4,1)} %iota_compare_fusion) | copy-start | bytes 786436
  674.5 1592.3 %all-reduce.5.cloned.1.call-start = ((), (), s32[]{:S(2)}) async-start(), calls=%async_computation.1 | async-start | bytes 83886080 | tf_op jit(solution)/shard_map/psum | solution.py:64
  1198.5 16.0 copy-start.13
  1198.5 16.0 copy-start.14
  1214.5 96.1 %copy-start.1 = (f32[512,64]{0,1:T(8,128)S(1)}, f32[512,64]{0,1:T(8,128)}, u32[]{:S(2)}) copy-start(f32[512,64]{0,1:T(8,128)} %get-tuple-element.25) | copy-start | bytes 393220
  1214.5 96.1 %copy-start.4 = (f32[512,64]{0,1:T(8,128)S(1)}, f32[512,64]{0,1:T(8,128)}, u32[]{:S(2)}) copy-start(f32[512,64]{0,1:T(8,128)} %get-tuple-element.26) | copy-start | bytes 393220
  1327.4 132.3 %copy-start.2 = (f32[512,64]{0,1:T(8,128)S(1)}, f32[512,64]{0,1:T(8,128)}, u32[]{:S(2)}) copy-start(f32[512,64]{0,1:T(8,128)} %get-tuple-element.25) | copy-start | bytes 393220
  1327.4 132.3 %copy-start.5 = (f32[512,64]{0,1:T(8,128)S(1)}, f32[512,64]{0,1:T(8,128)}, u32[]{:S(2)}) copy-start(f32[512,64]{0,1:T(8,128)} %get-tuple-element.26) | copy-start | bytes 393220
  1327.4 137.3 %copy-start.6 = (bf16[8,512,5,64]{1,3,2,0:T(8,128)(2,1)S(1)}, bf16[8,512,5,64]{1,3,2,0:T(8,128)(2,1)}, u32[]{:S(2)}) copy-start(bf16[8,512,5,64]{1,3,2,0:T(8,128)(2,1)} %get-tuple-element.13) | copy-start | bytes 7864324
  1327.4 137.3 %copy-start.8 = (pred[512,512]{0,1:T(8,128)(4,1)S(1)}, pred[512,512]{0,1:T(8,128)(4,1)}, u32[]{:S(2)}) copy-start(pred[512,512]{0,1:T(8,128)(4,1)} %iota_compare_fusion) | copy-start | bytes 786436
  1522.5 42.0 %copy-start.9 = (u8[512,2560]{1,0:T(8,128)(4,1)S(1)}, u8[512,2560]{1,0:T(8,128)(4,1)}, u32[]{:S(2)}) copy-start(u8[512,2560]{1,0:T(8,128)(4,1)} %get-tuple-element.5) | copy-start | bytes 3932164
  1522.5 42.0 %copy-start.10 = (u8[512,2560]{1,0:T(8,128)(4,1)S(1)}, u8[512,2560]{1,0:T(8,128)(4,1)}, u32[]{:S(2)}) copy-start(u8[512,2560]{1,0:T(8,128)(4,1)} %get-tuple-element.6) | copy-start | bytes 3932164
Sparse Core Ops, SparseCore 0:
  674.6 482.7 all-reduce.2
  1786.8 479.9 all-reduce.4
where the time goes:
time: 2320 us
  waiting for transfers between devices  937 us (40%)
  matrix products  871 us (38%)
  other arithmetic  388 us (17%)
  local copies, waits for them, and re-layouts  105 us (5%)
    psum x2, waiting for transfers between devices, shard_body(): reduced = lax.psum(local_sum, 'tp')  937 us
    dot_general x2, matrix products, layer_partial(): jnp.einsum('bsd,df->bsf', normed, w_up, preferred_element_type=jnp.float32)  264 us
    dot_general x2, matrix products, layer_partial(): jnp.einsum('bsf,fe->bse', gelu_out, w_down, preferred_element_type=jnp.fl...  249 us
    dot_general x2, other arithmetic, layer_partial(): jnp.einsum('bsf,fe->bse', gelu_out, w_down, preferred_element_type=jnp.fl...  195 us
    dot_general x2, matrix products, layer_partial(): jnp.einsum('bsd,dgc->bsgc', normed, w_qkv, preferred_element_type=jnp.flo...  193 us
    dot_general x2, matrix products, layer_partial(): jnp.einsum('bgrsd,grde->bse', context, out_heads, preferred_element_type=...  84 us
    dot_general x3, local copies, waits for them, and re-layouts, layer_partial(): jnp.einsum('bsd,dgc->bsgc', normed, w_qkv, preferred_element_type=jnp.flo...  77.8 us
    reduce_sum x2, other arithmetic, layer_norm(): row_mean = jnp.mean(hidden_f, axis=-1, keepdims=True)  54.8 us
  transfers between devices with their start and end apart: 2, of which 2 were waited for; matrix products, arithmetic and copies ran while one was open for 1% of the time, Pallas kernels for 0%

commit v1 on v0

v1 whole, which is shorter than its diff:
```python
import functools

import jax
import jax.numpy as jnp
from jax import lax
from jax.experimental import pallas as pl
from jax.experimental.pallas import tpu as pltpu
from jax.sharding import PartitionSpec as P

LN_EPS = 1e-5
ROPE_BASE = 10000.0
HEAD = 128
TILE = 512
F32 = jnp.float32
BF16 = jnp.bfloat16
VMEM_LIMIT = 66_500_000
COMM = True


def layer_norm(rows, gain, bias):
    rows = rows.astype(F32)
    centered = rows - jnp.mean(rows, axis=-1, keepdims=True)
    row_var = jnp.mean(centered * centered, axis=-1, keepdims=True)
    return (centered * lax.rsqrt(row_var + LN_EPS) * gain + bias).astype(BF16)


def gelu(val):
    return 0.5 * val * (1.0 + lax.erf(val * (0.5 ** 0.5)))


def rope_tables(seq_len):
    half = HEAD // 2
    inv_freq = ROPE_BASE ** (-2.0 * jnp.arange(half, dtype=F32) / HEAD)
    angles = jnp.arange(seq_len, dtype=F32)[:, None] * inv_freq[None, :]
    cos, sin = jnp.cos(angles), jnp.sin(angles)
    ones, zeros = jnp.ones((seq_len, HEAD), F32), jnp.zeros((seq_len, HEAD), F32)
    cos_tab = jnp.stack([jnp.concatenate([cos, cos], -1), ones])
    sin_tab = jnp.stack([jnp.concatenate([-sin, sin], -1), zeros])
    return cos_tab, sin_tab


def head_context(query, keys, values, scale):
    scores = lax.dot_general(query, keys, (((1,), (1,)), ((), ())), preferred_element_type=F32)
    rows, cols = scores.shape
    row_ids = lax.broadcasted_iota(jnp.int32, (rows, cols), 0) + (cols - rows)
    col_ids = lax.broadcasted_iota(jnp.int32, (rows, cols), 1)
    scores = jnp.where(row_ids >= col_ids, scores, -1e30)
    top = jnp.max(scores, axis=-1, keepdims=True)
    weights = jnp.exp((scores - top) * scale)
    probs = weights * (1.0 / jnp.sum(weights, axis=-1, keepdims=True))
    return jnp.dot(probs.astype(BF16), values, preferred_element_type=F32).astype(BF16)


def mega_kernel(seqs, heads, x_hbm, gain_ref, bias_ref, cos_ref, sin_ref, wq_hbm, wo_hbm, wu_hbm, wd_hbm, g_hbm,
                norm, w_a, w_b, mid, qkv, part, pair, rs1, rs2, resid, shard,
                sem_a, sem_b, sem_x, sem_pair_s, sem_pair_r, sem_res, sem_loc,
                rs1_s, rs1_r, rs2_s, rs2_r, ag1_s, ag1_r, ag2_s, ag2_r, fin_s, fin_r):
    layers = wq_hbm.shape[0]
    d_model = wq_hbm.shape[2]
    seq_len = x_hbm.shape[1]
    steps = layers * seqs
    q_blocks = 3 * heads
    q_tiles = (q_blocks * HEAD + TILE - 1) // TILE
    attn_width = heads * HEAD
    ups = heads
    downs = 5
    t_down = d_model // downs
    half = seq_len // 2
    sub = half // 2
    q32 = sub // 4
    q16 = sub // 8
    ln_rows = seq_len // (downs - 1)
    scale = HEAD ** -0.5

    me = lax.axis_index("tp")
    core = me % 2
    x_pos = (me // 2) % 2
    y_pos = me // 4
    partner = me + 1 - 2 * core
    x_nbr = me + 2 - 4 * x_pos
    y_nbr = me + 4 - 8 * y_pos

    def remote(src, dst, s_sem, r_sem, target):
        return pltpu.make_async_remote_copy(src_ref=src, dst_ref=dst, send_sem=s_sem, recv_sem=r_sem,
                                            device_id={"tp": target}, device_id_type=pl.DeviceIdType.MESH)

    local = pltpu.make_async_copy

    def start_q(layer, tile, slot):
        for k in range(TILE // HEAD):
            blk = jnp.minimum(tile * (TILE // HEAD) + k, q_blocks - 1)
            col = pl.multiple_of((blk % 3) * HEAD, HEAD)
            local(wq_hbm.at[layer, blk // 3, :, pl.ds(col, HEAD)], w_a.at[slot, :, pl.ds(k * HEAD, HEAD)], sem_a.at[slot]).start()

    def start_u(layer, tile, slot):
        col = pl.multiple_of(tile * TILE, TILE)
        local(wu_hbm.at[layer, :, pl.ds(col, TILE)], w_a.at[slot], sem_a.at[slot]).start()

    def wait_a(slot):
        local(wu_hbm.at[0, :, pl.ds(0, TILE)], w_a.at[slot], sem_a.at[slot]).wait()

    def start_b(layer, tile, slot):
        col = pl.multiple_of(tile * t_down, t_down)
        local(wo_hbm.at[layer, :, pl.ds(col, t_down)], w_b.at[slot, pl.ds(0, attn_width)], sem_b.at[slot, 0]).start()
        local(wd_hbm.at[layer, :, pl.ds(col, t_down)], w_b.at[slot, pl.ds(attn_width, wd_hbm.shape[1])], sem_b.at[slot, 1]).start()

    def wait_b(slot):
        local(wo_hbm.at[0, :, pl.ds(0, t_down)], w_b.at[slot, pl.ds(0, attn_width)], sem_b.at[slot, 0]).wait()
        local(wd_hbm.at[0, :, pl.ds(0, t_down)], w_b.at[slot, pl.ds(attn_width, wd_hbm.shape[1])], sem_b.at[slot, 1]).wait()

    def start_x(step):
        @pl.when(step < seqs)
        def _():
            local(x_hbm.at[step], norm.at[pl.ds(0, seq_len)], sem_x).start()

        @pl.when(step >= seqs)
        def _():
            local(g_hbm.at[jnp.maximum(step - seqs, 0)], norm.at[pl.ds(0, seq_len)], sem_x).start()

    def wait_x():
        local(x_hbm.at[0], norm.at[pl.ds(0, seq_len)], sem_x).wait()

    def norm_block(layer, blk):
        rows = pl.ds(pl.multiple_of(blk * ln_rows, ln_rows), ln_rows)
        norm[rows, :] = layer_norm(norm[rows, :], gain_ref[layer], bias_ref[layer])

    base = core * half

    def keep32(u, colour):
        pos = x_pos if colour == 0 else y_pos
        return u * sub + colour * (sub // 2) + pos * q32

    def send32(u, colour):
        pos = x_pos if colour == 0 else y_pos
        return u * sub + colour * (sub // 2) + (1 - pos) * q32

    def keep16(u, colour):
        pos = y_pos if colour == 0 else x_pos
        return keep32(u, colour) + pos * q16

    def send16(u, colour):
        pos = y_pos if colour == 0 else x_pos
        return keep32(u, colour) + (1 - pos) * q16

    first_nbr = (x_nbr, y_nbr)
    second_nbr = (y_nbr, x_nbr)

    def al(val):
        return pl.multiple_of(val, q16)

    def pair_copy(slot, tile):
        cols = pl.ds(pl.multiple_of(tile * t_down, t_down), t_down)
        src = part.at[pl.ds(pl.multiple_of((1 - core) * half, half), half), cols]
        return remote(src, pair.at[slot, :, cols], sem_pair_s.at[slot], sem_pair_r.at[slot], partner)

    def rs1_copy(slot, u, k):
        return remote(pair.at[slot, pl.ds(al(send32(u, k)), q32)], rs1.at[u, k], rs1_s.at[u, k], rs1_r.at[u, k], first_nbr[k])

    def rs2_copy(slot, u, k):
        return remote(pair.at[slot, pl.ds(al(send16(u, k)), q16)], rs2.at[u, k], rs2_s.at[u, k], rs2_r.at[u, k], second_nbr[k])

    def g_rows(seq, start, size):
        return g_hbm.at[seq, pl.ds(al(base + start), size)]

    def ag1_copy(seq, u, k):
        return remote(shard.at[u, k], g_rows(seq, keep16(u, k), q16), ag1_s.at[u, k], ag1_r.at[u, k], second_nbr[k])

    def ag2_copy(seq, u, k):
        rows = g_rows(seq, keep32(u, k), q32)
        return remote(rows, rows, ag2_s.at[u, k], ag2_r.at[u, k], first_nbr[k])

    def fin_copy(seq, u):
        rows = g_rows(seq, u * sub, sub)
        return remote(rows, rows, fin_s.at[lax.rem(seq, 2), u], fin_r.at[lax.rem(seq, 2), u], partner)

    def res_copy(src, seq, u, k):
        return local(src.at[seq, pl.ds(al(base + keep16(u, k)), q16)], resid.at[u, k], sem_res.at[u, k])

    def loc_copy(seq, u, k):
        return local(shard.at[u, k], g_rows(seq, keep16(u, k), q16), sem_loc.at[u, k])

    pairs = [(u, k) for u in range(2) for k in range(2)]

    def reduce_pair(seq):
        slot = seq % 2
        whole = part.at[pl.ds(0, half)]
        remote(whole, pair.at[slot], sem_pair_s.at[slot], sem_pair_r.at[slot], partner).wait()

        @pl.loop(0, half // q32)
        def _(i):
            rows = pl.ds(pl.multiple_of(i * q32, q32), q32)
            mine = part[pl.ds(pl.multiple_of(core * half + i * q32, q32), q32), :].astype(F32)
            pair[slot, rows, :] = (mine + pair[slot, rows, :].astype(F32)).astype(BF16)

        for u, k in pairs:
            rs1_copy(slot, u, k).start()

        for u, k in pairs:
            @pl.when(seq < seqs)
            def _():
                res_copy(x_hbm, seq, u, k).start()

            @pl.when(seq >= seqs)
            def _():
                res_copy(g_hbm, jnp.maximum(seq - seqs, 0), u, k).start()

    def reduce_first(seq, u):
        slot = seq % 2
        for k in range(2):
            rs1_copy(slot, u, k).wait()
            rows = pl.ds(al(keep32(u, k)), q32)
            pair[slot, rows, :] = (pair[slot, rows, :].astype(F32) + rs1[u, k].astype(F32)).astype(BF16)
        for k in range(2):
            rs2_copy(slot, u, k).start()

    def reduce_second(seq, u):
        slot = seq % 2
        for k in range(2):
            rs2_copy(slot, u, k).wait()
            res_copy(x_hbm, 0, u, k).wait()
            rows = pl.ds(al(keep16(u, k)), q16)
            update = (pair[slot, rows, :].astype(F32) + rs2[u, k].astype(F32)).astype(BF16)
            shard[u, k] = (resid[u, k].astype(F32) + update.astype(F32)).astype(BF16)
        for k in range(2):
            loc_copy(seq, u, k).start()
            ag1_copy(seq, u, k).start()

    def gather_first(seq, u):
        for k in range(2):
            loc_copy(seq, u, k).wait()
            ag1_copy(seq, u, k).wait()
        for k in range(2):
            ag2_copy(seq, u, k).start()

    def gather_pair(seq, u):
        for k in range(2):
            ag2_copy(seq, u, k).wait()
        fin_copy(seq, u).start()

    def gather_done(seq):
        for u in range(2):
            fin_copy(seq, u).wait()

    if COMM:
        barrier = pltpu.get_barrier_semaphore()
        for nbr in (partner, x_nbr, y_nbr):
            pl.semaphore_signal(barrier, inc=1, device_id={"tp": nbr}, device_id_type=pl.DeviceIdType.MESH)
        pl.semaphore_wait(barrier, 3)
    start_x(0)
    start_q(0, 0, 0)
    start_q(0, 1, 1)
    wait_x()

    @pl.loop(0, downs - 1)
    def _(blk):
        norm_block(0, blk)

    def when_comm(cond):
        if COMM:
            return pl.when(cond)
        return lambda fn: None

    @pl.loop(0, steps)
    def _(step):
        layer = step // seqs
        prev = step - 1
        has_prev = step >= 1

        @pl.loop(0, q_tiles)
        def _(i):
            nxt = lax.rem(i + 2, 3)

            @pl.when(i + 2 < q_tiles)
            def _():
                start_q(layer, i + 2, nxt)

            @pl.when(i + 2 >= q_tiles)
            def _():
                start_u(layer, i + 2 - q_tiles, nxt)

            slot = lax.rem(i, 3)
            wait_a(slot)
            prod = jnp.dot(norm[pl.ds(0, seq_len), :], w_a[slot], preferred_element_type=F32)
            for k in range(TILE // HEAD):
                blk = prod[:, k * HEAD:(k + 1) * HEAD]
                kind = (i * (TILE // HEAD) + k) % 3 // 2
                turned = blk * cos_ref[kind] + pltpu.roll(blk, HEAD // 2, 1) * sin_ref[kind]
                col = pl.multiple_of(i * TILE + k * HEAD, HEAD)
                qkv[:, pl.ds(col, HEAD)] = turned.astype(BF16)

            @when_comm((i == 0) & has_prev)
            def _():
                reduce_pair(prev)

            @when_comm((i == 1) & (step >= 2))
            def _():
                gather_pair(prev - 1, 1)

            @when_comm((i == 3) & (step >= 2))
            def _():
                gather_done(prev - 1)

            @when_comm((i == 3) & has_prev)
            def _():
                reduce_first(prev, 0)

        start_b(layer, 0, lax.rem(step * downs, 2))

        @pl.loop(0, ups)
        def _(j):
            a = q_tiles + j
            nxt = lax.rem(a + 2, 3)

            @pl.when(j + 2 < ups)
            def _():
                start_u(layer, j + 2, nxt)

            @pl.when((j + 2 >= ups) & (step + 1 < steps))
            def _():
                start_q((step + 1) // seqs, j + 2 - ups, nxt)

            slot = lax.rem(a, 3)
            wait_a(slot)
            prod = jnp.dot(norm[pl.ds(0, seq_len), :], w_a[slot], preferred_element_type=F32)
            mid[:, pl.ds(pl.multiple_of(attn_width + j * TILE, HEAD), TILE)] = gelu(prod).astype(BF16)
            q_cols = pl.ds(pl.multiple_of(j * 3 * HEAD, HEAD), HEAD)
            k_cols = pl.ds(pl.multiple_of(j * 3 * HEAD + HEAD, HEAD), HEAD)
            v_cols = pl.ds(pl.multiple_of(j * 3 * HEAD + 2 * HEAD, HEAD), HEAD)
            o_cols = pl.ds(pl.multiple_of(j * HEAD, HEAD), HEAD)
            for blk in range(2):
                rows = pl.ds(blk * half, half)
                seen = pl.ds(0, (blk + 1) * half)
                mid[rows, o_cols] = head_context(qkv[rows, q_cols], qkv[seen, k_cols], qkv[seen, v_cols], scale)

            @when_comm((j == 1) & has_prev)
            def _():
                reduce_first(prev, 1)

            @when_comm((j == 3) & has_prev)
            def _():
                reduce_second(prev, 0)

            @when_comm((j == 4) & has_prev)
            def _():
                reduce_second(prev, 1)

        @pl.loop(0, downs)
        def _(j):
            slot = lax.rem(step * downs + j, 2)

            @pl.when(j + 1 < downs)
            def _():
                start_b(layer, j + 1, 1 - slot)

            @pl.when((j == 0) & (step + 1 < steps))
            def _():
                start_x(step + 1)

            @pl.when((j == 1) & (step + 1 < steps))
            def _():
                wait_x()

            wait_b(slot)
            prod = jnp.dot(mid[...], w_b[slot], preferred_element_type=F32)
            part[:, pl.ds(pl.multiple_of(j * t_down, t_down), t_down)] = prod.astype(BF16)
            norm_block(jnp.minimum((step + 1) // seqs, layers - 1), (j + downs - 1) % downs)
            if COMM:
                pair_copy(lax.rem(step, 2), j).start()

            @when_comm((j == 0) & has_prev)
            def _():
                gather_first(prev, 0)

            @when_comm((j == 1) & has_prev)
            def _():
                gather_first(prev, 1)

            @when_comm((j == 3) & has_prev)
            def _():
                gather_pair(prev, 0)

    if COMM:
        last = steps - 1
        reduce_pair(last)
        gather_pair(last - 1, 1)
        gather_done(last - 1)
        for u in range(2):
            reduce_first(last, u)
        for u in range(2):
            reduce_second(last, u)
        for u in range(2):
            gather_first(last, u)
        for u in range(2):
            gather_pair(last, u)
        gather_done(last)
    else:
        cp = local(part, g_hbm.at[0], sem_x)
        cp.start()
        cp.wait()


def mega_call(x, gain, bias, w_qkv, w_out, w_up, w_down):
    seqs, seq_len, d_model = x.shape
    layers, _, heads, _ = w_qkv.shape
    w_q = jnp.transpose(w_qkv, (0, 2, 1, 3))
    cos_tab, sin_tab = rope_tables(seq_len)
    mid_width = heads * HEAD + w_down.shape[1]
    half = seq_len // 2
    sub = half // 2
    t_down = d_model // 5
    q_cols = -(-3 * heads * HEAD // TILE) * TILE
    any_spec = pl.BlockSpec(memory_space=pl.ANY)
    vmem_spec = pl.BlockSpec(memory_space=pltpu.VMEM)
    dma = pltpu.SemaphoreType.DMA
    flops = 2 * layers * seqs * seq_len * d_model * (3 * heads * HEAD + w_up.shape[2] + mid_width)
    return pl.pallas_call(
        functools.partial(mega_kernel, seqs, heads),
        out_shape=jax.ShapeDtypeStruct((layers * seqs, seq_len, d_model), BF16),
        in_specs=[any_spec, vmem_spec, vmem_spec, vmem_spec, vmem_spec, any_spec, any_spec, any_spec, any_spec],
        out_specs=any_spec,
        scratch_shapes=[
            pltpu.VMEM((seq_len + seq_len // 4, d_model), BF16),
            pltpu.VMEM((3, d_model, TILE), BF16),
            pltpu.VMEM((2, mid_width, t_down), BF16),
            pltpu.VMEM((seq_len, mid_width), BF16),
            pltpu.VMEM((seq_len, q_cols), BF16),
            pltpu.VMEM((seq_len, d_model), BF16),
            pltpu.VMEM((2, half, d_model), BF16),
            pltpu.VMEM((2, 2, sub // 4, d_model), BF16),
            pltpu.VMEM((2, 2, sub // 8, d_model), BF16),
            pltpu.VMEM((2, 2, sub // 8, d_model), BF16),
            pltpu.VMEM((2, 2, sub // 8, d_model), BF16),
            dma((3,)), dma((2, 2)), dma, dma((2,)), dma((2,)), dma((2, 2)), dma((2, 2)),
            dma((2, 2)), dma((2, 2)), dma((2, 2)), dma((2, 2)),
            dma((2, 2)), dma((2, 2)), dma((2, 2)), dma((2, 2)), dma((2, 2)), dma((2, 2)),
        ],
        compiler_params=pltpu.CompilerParams(collective_id=0 if COMM else None, has_side_effects=True, vmem_limit_bytes=VMEM_LIMIT),
        cost_estimate=pl.CostEstimate(flops=flops, bytes_accessed=flops // 500, transcendentals=0),
        name="layers",
    )(x, gain[:, None, :], bias[:, None, :], cos_tab, sin_tab, w_q, w_out, w_up, w_down)


def solution(mesh):
    def shard_body(x, gain, bias, w_qkv, w_out, w_up, w_down):
        gathered = mega_call(x, gain, bias, w_qkv, w_out, w_up, w_down)
        return gathered[gathered.shape[0] - x.shape[0]:]

    return jax.shard_map(shard_body, mesh=mesh, in_specs=(P("dp", None, None), P(None, None), P(None, None), P(None, None, "tp", None), P(None, "tp", None), P(None, None, "tp"), P(None, "tp", None)), out_specs=P("dp", None, None), check_vma=False)
```

time: 2320 us -> 992 us (0.43)
  Pallas kernels: 0 us -> 958 us
  waiting for transfers between devices: 937 us -> 0 us
  matrix products: 871 us -> 0 us
  other arithmetic: 388 us -> 1.21 us
  local copies, waits for them, and re-layouts: 105 us -> 32.7 us
    pallas_call x0 -> x1, Pallas kernels: none -> 958 us  [mega_call(): pl.pallas_call(functools.partial(mega_kernel, seqs, heads), out_shape=jax...]
    psum x2 -> x0, waiting for transfers between devices: 937 us -> none  [shard_body(): reduced = lax.psum(local_sum, 'tp')]
    dot_general x12 -> x0, matrix products: 871 us -> none  [the longest x2 264 us: layer_partial(): jnp.einsum('bsd,df->bsf', normed, w_up, preferred_element_type=jnp.float32)]
    dot_general x2 -> x0, other arithmetic: 195 us -> none  [layer_partial(): jnp.einsum('bsf,fe->bse', gelu_out, w_down, preferred_element_type=jnp.fl...]
    reduce_sum x6 -> x0, other arithmetic: 122 us -> none  [the longest x2 54.8 us: layer_norm(): row_mean = jnp.mean(hidden_f, axis=-1, keepdims=True)]
    dot_general x3 -> x0, local copies, waits for them, and re-layouts: 77.8 us -> none  [layer_partial(): jnp.einsum('bsd,dgc->bsgc', normed, w_qkv, preferred_element_type=jnp.flo...]
    convert_element_type x1 -> x0, other arithmetic: 41.4 us -> none  [shard_body(): (hidden.astype(jnp.float32) + reduced.astype(jnp.float32)).astype(jnp.bfl...]
  transfers between devices with their start and end apart: 2 -> 0, of which waited for: 2 -> 0; matrix products, arithmetic and copies ran while one was open for 1% -> 0% of each run, Pallas kernels for 0% -> 0%
where the time goes in v1:
time: 992 us; the launch traced here: 991 us
  Pallas kernels  958 us (97%)
  local copies, waits for them, and re-layouts  32.7 us (3%)
    pallas_call x1, Pallas kernels, mega_call(): pl.pallas_call(functools.partial(mega_kernel, seqs, heads), out_shape=jax...  958 us
    slice x1, local copies, waits for them, and re-layouts, shard_body(): return gathered[gathered.shape[0] - x.shape[0]:]  28.2 us

profile of v1, /device:TPU:0, one launch (start us, length us, event | category | flops | bytes accessed | tf_op | source)
XLA Modules:
  0.0 991.5 jit_solution(5175253462948007782)
XLA Ops:
  0.0 1.4 broadcast_in_dim.8.gain_ref
  1.4 1.4 broadcast_in_dim.9.bias_ref
  2.8 1.0 fusion.2
  3.8 0.2 maximum_bitcast_fusion
  4.0 0.8 stack.13.cos_ref
  4.9 0.8 stack.15.sin_ref
  5.7 957.5 %layers.1 = bf16[16,512,5120]{2,1,0:T(8,128)(2,1)} custom-call(bf16[8,512,5120]{2,1,0:T(8,128)(2,1)} %x_hbm.1, f32[2,1,5120]{2,1,0:T(1,128)} %broadcast_in_dim.8.gain_ref, f32[2,1,5120]{2,1,0:T(1,128)} %broadcast_in_dim.9.bias_ref, f32[2,512,128]{2,1,0:T(8,128)} %stack.13.cos_ref, f32[2,512,128]{2,1,0:T(8,128)} %stack.15.sin_ref, ...), custom_call_target="tpu_custom_call" | custom-call | flops 644245094400 | bytes 1288490240 | tf_op jit(solution)/shard_map/layers/pallas_call | solution.py:416
  963.3 28.2 %slice.3 = bf16[8,512,5120]{2,1,0:T(8,128)(2,1)} slice(bf16[16,512,5120]{2,1,0:T(8,128)(2,1)} %layers.1), slice={[8:16], [0:512], [0:5120]} | slice | bytes 83886080 | tf_op jit(solution)/shard_map/slice | solution.py:446
  (1 shorter events, 0.0 us)
